TPU v7x, 32 devices: a whole 2x2x4 slice. The times are simulated.
32 devices in a mesh: gx: 2 (over y), gy: 4 (over x, core), gz: 4 (over z).
Axes of the slice: x: 2, y: 2, z: 4, core: 2. Of those that a mesh axis runs over, the one named last changes fastest.
Arguments:
- volume: float32 [16, 64, 512], P(('gx', 'gy'), None, 'gz'), may hold values from 0 to 1
- levels: int32 [4], replicated, may hold values from 0 to 255
Outputs:
- labelling: float32 [4, 16, 64, 512], P(None, 'gx', 'gy', 'gz')
- centers: float32 [4], replicated
All inputs are finite; a program needn't handle non-finite values.
Results may differ from a plain program's by a relative error of at most 0.0001.
Values sent between devices are 32-bit elements; how exact they have to be, the bound alone decides.
A program may use at most 64 MiB of HBM per device.

v0:
```python
import jax
import jax.numpy as jnp
from jax import lax
from jax.sharding import PartitionSpec as P

ITERS = 2
tau_step = 0.25
sigma_step = 0.25
smooth_weight = 0.5
prior_weight = 1.0


def with_halo(block, sides, width):
    for axis, dim in sides:
        count = lax.axis_size(axis)
        forward = [(i, i + 1) for i in range(count - 1)]
        backward = [(target, source) for source, target in forward]
        low = lax.ppermute(
            lax.slice_in_dim(block, block.shape[dim] - width, None, axis=dim), axis, forward
        )
        high = lax.ppermute(lax.slice_in_dim(block, 0, width, axis=dim), axis, backward)
        block = jnp.concatenate([low, block, high], axis=dim)
    return block


def project_simplex(values):
    how_many = values.shape[0]
    threshold = None
    for subset in range(1, 1 << how_many):
        members = [label_index for label_index in range(how_many) if subset >> label_index & 1]
        summed = values[members[0]]
        for label_index in members[1:]:
            summed = summed + values[label_index]
        candidate = (summed - 1.0) / float(len(members))
        threshold = candidate if threshold is None else jnp.maximum(threshold, candidate)
    return jnp.maximum(values - threshold[None], 0.0)


def bounds(start, total, extent):
    position = start - 1 + jnp.arange(extent + 1, dtype=jnp.int32)
    return (position >= 0, position < total - 1)


def local(volume, levels):
    thickness = volume.shape[0]
    x_start = (lax.axis_index("gx") * lax.axis_size("gy") + lax.axis_index("gy")) * thickness
    x_total = thickness * lax.axis_size("gx") * lax.axis_size("gy")
    y_start = 0
    y_total = volume.shape[1]
    z_start = lax.axis_index("gz") * volume.shape[2]
    z_total = volume.shape[2] * lax.axis_size("gz")
    extent = volume.shape
    how_many = levels.shape[0]
    inside_x, ahead_x = bounds(x_start, x_total, extent[0])
    inside_y, ahead_y = bounds(y_start, y_total, extent[1])
    inside_z, ahead_z = bounds(z_start, z_total, extent[2])
    inside = (inside_x[:, None, None] & inside_y[None, :, None] & inside_z[None, None, :]).astype(
        jnp.float32
    )
    base_levels = levels.astype(jnp.float32) / 255.0
    centers = base_levels
    starting = (volume[None] - base_levels[:, None, None, None]) ** 2
    labelling = project_simplex(1.0 / how_many - tau_step * starting)
    smoothed = labelling
    dual_field = jnp.zeros((how_many, 3, extent[0] + 1, extent[1] + 1, extent[2] + 1), jnp.float32)
    for iteration in range(ITERS):
        padded = with_halo(smoothed, ((("gx", "gy"), 1), ("gz", 3)), 1)
        padded = jnp.pad(padded, ((0, 0), (0, 0), (1, 1), (0, 0)))
        corner = padded[:, :-1, :-1, :-1]
        grad_x = jnp.where(ahead_x[:, None, None], padded[:, 1:, :-1, :-1] - corner, 0.0)
        grad_y = jnp.where(ahead_y[None, :, None], padded[:, :-1, 1:, :-1] - corner, 0.0)
        grad_z = jnp.where(ahead_z[None, None, :], padded[:, :-1, :-1, 1:] - corner, 0.0)
        stepped = dual_field + sigma_step * jnp.stack([grad_x, grad_y, grad_z], axis=1)
        length = jnp.sqrt(
            stepped[:, 0] * stepped[:, 0]
            + stepped[:, 1] * stepped[:, 1]
            + stepped[:, 2] * stepped[:, 2]
        )
        shrink = inside / jnp.maximum(1.0, length / smooth_weight)
        dual_field = stepped * shrink[:, None]
        divergence = (
            dual_field[:, 0, 1:, 1:, 1:]
            - dual_field[:, 0, :-1, 1:, 1:]
            + (dual_field[:, 1, 1:, 1:, 1:] - dual_field[:, 1, 1:, :-1, 1:])
            + (dual_field[:, 2, 1:, 1:, 1:] - dual_field[:, 2, 1:, 1:, :-1])
        )
        fidelity = (volume[None] - centers[:, None, None, None]) ** 2
        updated = project_simplex(labelling + tau_step * (divergence - fidelity))
        smoothed = 2.0 * updated - labelling
        labelling = updated
        sizes_local = jnp.sum(labelling, axis=(1, 2, 3))
        weighted = jnp.sum(labelling * volume[None], axis=(1, 2, 3))
        sizes_all, weighted_all = lax.psum((sizes_local, weighted), ("gx", "gy", "gz"))
        centers = (weighted_all + prior_weight * base_levels) / (sizes_all + prior_weight)
    labelling = lax.all_to_all(labelling, "gy", split_axis=2, concat_axis=1, tiled=True)
    return (labelling, centers)


def solution(mesh):
    return jax.shard_map(
        local,
        mesh=mesh,
        in_specs=(P(("gx", "gy"), None, "gz"), P()),
        out_specs=(P(None, "gx", "gy", "gz"), P()),
        check_vma=False,
    )
```

profile of v0, /device:TPU:0, one launch (start us, length us, event | category | flops | bytes accessed | tf_op | source)
XLA Modules:
  0.0 159.2 jit_solution(3588290688517704985)
XLA Ops:
  0.6 0.7 convert_multiply_fusion
  1.3 0.9 multiply_subtract_fusion.1
  2.2 0.1 maximum_bitcast_fusion.2
  2.4 0.6 copy-done.8
  3.0 1.0 subtract_maximum_fusion.2
  4.0 2.4 %collective-permute-start = (f32[4,1,64,128]{3,2,1,0:T(8,128)S(1)}, f32[4,1,64,128]{3,2,1,0:T(8,128)S(1)}, u32[]{:S(2)}, u32[]{:S(2)}) collective-permute-start(f32[4,1,64,128]{3,2,1,0:T(8,128)S(1)} %get-tuple-element.24), channel_id=1, source_target_pairs={{0,4},{4,8},{8,12},{12,16},{16,20},{20,24},{24,28},{1,5},{5,9},{9,... | collective-permute-start | bytes 393224 | tf_op jit(solution)/shard_map/ppermute | solution.py:18
  6.4 1.3 collective-permute-start.1
  7.7 0.1 broadcast_and_fusion
  7.8 0.1 and_convert_fusion
  8.0 0.0 collective-permute-done
  8.0 3.7 %collective-permute-done.1 = f32[4,1,64,128]{3,2,1,0:T(8,128)S(1)} collective-permute-done((f32[4,1,64,128]{3,2,1,0:T(8,128)S(1)}, f32[4,1,64,128]{3,2,1,0:T(8,128)S(1)}, u32[]{:S(2)}, u32[]{:S(2)}) %collective-permute-start.1) | collective-permute-done | bytes 131104 | tf_op jit(solution)/shard_map/ppermute | solution.py:21
  11.8 0.2 fusion.66
  12.0 3.5 %collective-permute-start.2 = (f32[4,4,64,1]{3,2,1,0:T(8,128)S(1)}, f32[4,4,64,1]{3,2,1,0:T(8,128)S(1)}, u32[]{:S(2)}, u32[]{:S(2)}) collective-permute-start(f32[4,4,64,1]{3,2,1,0:T(8,128)S(1)} %get-tuple-element.19), channel_id=1, source_target_pairs={{0,1},{1,2},{2,3},{4,5},{5,6},{6,7},{8,9},{9,10},{10,11},{12,13},{... | collective-permute-start | bytes 12296 | tf_op jit(solution)/shard_map/ppermute | solution.py:18
  15.5 1.3 collective-permute-start.3
  16.8 8.4 %collective-permute-done.2 = f32[4,4,64,1]{3,2,1,0:T(8,128)S(1)} collective-permute-done((f32[4,4,64,1]{3,2,1,0:T(8,128)S(1)}, f32[4,4,64,1]{3,2,1,0:T(8,128)S(1)}, u32[]{:S(2)}, u32[]{:S(2)}) %collective-permute-start.2) | collective-permute-done | bytes 4128 | tf_op jit(solution)/shard_map/ppermute | solution.py:18
  25.2 4.7 %collective-permute-done.3 = f32[4,4,64,1]{3,2,1,0:T(8,128)S(1)} collective-permute-done((f32[4,4,64,1]{3,2,1,0:T(8,128)S(1)}, f32[4,4,64,1]{3,2,1,0:T(8,128)S(1)}, u32[]{:S(2)}, u32[]{:S(2)}) %collective-permute-start.3) | collective-permute-done | bytes 4128 | tf_op jit(solution)/shard_map/ppermute | solution.py:21
  29.9 0.5 select_maximum_fusion.4
  30.4 0.5 fusion.29
  30.9 0.2 fusion.2
  31.2 0.5 fusion.30
  31.7 0.0 copy-start.4
  31.7 0.0 copy-start.9
  31.7 0.3 fusion.1
  32.0 0.5 copy-done.4
  32.5 0.0 copy-done.9
  32.6 0.5 fusion.41
  33.0 0.1 maximum_bitcast_fusion.1
  33.1 0.9 copy-done
  34.1 1.1 multiply_reduce_fusion.1
  35.2 0.7 copy-done.2
  35.9 0.7 fusion.67
  36.6 4.7 %collective-permute-start.4 = (f32[4,1,64,128]{3,2,1,0:T(8,128)}, f32[4,1,64,128]{3,2,1,0:T(8,128)}, u32[]{:S(2)}, u32[]{:S(2)}) collective-permute-start(f32[4,1,64,128]{3,2,1,0:T(8,128)} %get-tuple-element.22), channel_id=1, source_target_pairs={{0,4},{4,8},{8,12},{12,16},{16,20},{20,24},{24,28},{1,5},{5,9},{9,... | collective-permute-start | bytes 393224 | tf_op jit(solution)/shard_map/ppermute | solution.py:18
  41.3 1.3 collective-permute-start.5
  42.6 44.4 %all-reduce.3 = (f32[4]{0:T(128)}, f32[4]{0:T(128)}) all-reduce(f32[4]{0:T(128)} %get-tuple-element.3, f32[4]{0:T(128)} %get-tuple-element.2), channel_id=1, replica_groups=mesh['gx'=2,'gy'=4,'gz'=4] {'gx','gy','gz'}, use_global_device_ids=true, to_apply=%region_3.4 | all-reduce | flops 8 | bytes 64 | tf_op jit(solution)/shard_map/psum | solution.py:93
  87.0 0.0 collective-permute-done.4
  87.0 0.0 collective-permute-done.5
  87.0 1.1 pad_maximum_fusion.2
  88.2 0.2 fusion.65
  88.4 2.3 %collective-permute-start.6 = (f32[4,4,64,1]{3,2,1,0:T(8,128)S(1)}, f32[4,4,64,1]{3,2,1,0:T(8,128)S(1)}, u32[]{:S(2)}, u32[]{:S(2)}) collective-permute-start(f32[4,4,64,1]{3,2,1,0:T(8,128)S(1)} %get-tuple-element.17), channel_id=1, source_target_pairs={{0,1},{1,2},{2,3},{4,5},{5,6},{6,7},{8,9},{9,10},{10,11},{12,13},{... | collective-permute-start | bytes 12296 | tf_op jit(solution)/shard_map/ppermute | solution.py:18
  90.7 1.3 collective-permute-start.7
  92.0 0.0 copy-done.13
  92.0 0.0 copy-done.16
  92.1 0.0 copy-done.17
  92.1 9.2 %collective-permute-done.6 = f32[4,4,64,1]{3,2,1,0:T(8,128)S(1)} collective-permute-done((f32[4,4,64,1]{3,2,1,0:T(8,128)S(1)}, f32[4,4,64,1]{3,2,1,0:T(8,128)S(1)}, u32[]{:S(2)}, u32[]{:S(2)}) %collective-permute-start.6) | collective-permute-done | bytes 4128 | tf_op jit(solution)/shard_map/ppermute | solution.py:18
  101.3 4.1 %collective-permute-done.7 = f32[4,4,64,1]{3,2,1,0:T(8,128)S(1)} collective-permute-done((f32[4,4,64,1]{3,2,1,0:T(8,128)S(1)}, f32[4,4,64,1]{3,2,1,0:T(8,128)S(1)}, u32[]{:S(2)}, u32[]{:S(2)}) %collective-permute-start.7) | collective-permute-done | bytes 4128 | tf_op jit(solution)/shard_map/ppermute | solution.py:21
  105.5 1.5 select_maximum_fusion
  107.0 0.4 fusion.16
  107.4 0.4 fusion
  107.9 0.5 copy-done.7
  108.3 0.5 fusion.9
  108.8 0.0 copy-start.5
  108.8 0.0 copy-start.10
  108.9 0.5 broadcast_multiply_fusion
  109.4 1.2 copy-done.1
  110.6 0.8 fusion.35
  111.4 0.1 maximum_bitcast_fusion
  111.5 0.2 multiply_reduce_fusion
  111.6 0.9 copy.8
  112.5 3.9 %all-to-all-start = ((f32[4,2,64,128]{3,1,0,2:T(2,128)}), f32[4,2,64,128]{3,1,0,2:T(2,128)S(1)}, u32[]{:S(2)}, u32[]{:S(2)}) async-start(f32[4,2,64,128]{3,1,0,2:T(2,128)} %copy.8), calls=%async_computation | async-start | bytes 524288 | tf_op jit(solution)/shard_map/all_to_all | solution.py:95
  116.4 41.5 %all-reduce.2 = (f32[4]{0:T(128)S(1)}, f32[4]{0:T(128)S(1)}) all-reduce(f32[4]{0:T(128)S(1)} %get-tuple-element.5, f32[4]{0:T(128)S(1)} %get-tuple-element.4), channel_id=1, replica_groups=mesh['gx'=2,'gy'=4,'gz'=4] {'gx','gy','gz'}, use_global_device_ids=true, to_apply=%region_7.8 | all-reduce | flops 8 | bytes 64 | tf_op jit(solution)/shard_map/psum | solution.py:93
  157.9 0.5 add_divide_fusion
  158.4 0.0 all-to-all-done
  158.4 0.1 copy.9
  158.5 0.7 copy.10
  (31 shorter events, 0.2 us)
Async XLA Ops:
  2.4 0.6 copy-start.8
  4.0 4.0 %collective-permute-start = (f32[4,1,64,128]{3,2,1,0:T(8,128)S(1)}, f32[4,1,64,128]{3,2,1,0:T(8,128)S(1)}, u32[]{:S(2)}, u32[]{:S(2)}) collective-permute-start(f32[4,1,64,128]{3,2,1,0:T(8,128)S(1)} %get-tuple-element.24), channel_id=1, source_target_pairs={{0,4},{4,8},{8,12},{12,16},{16,20},{20,24},{24,28},{1,5},{5,9},{9,... | collective-permute-start | bytes 393224 | tf_op jit(solution)/shard_map/ppermute | solution.py:18
  6.4 5.3 %collective-permute-start.1 = (f32[4,1,64,128]{3,2,1,0:T(8,128)S(1)}, f32[4,1,64,128]{3,2,1,0:T(8,128)S(1)}, u32[]{:S(2)}, u32[]{:S(2)}) collective-permute-start(f32[4,1,64,128]{3,2,1,0:T(8,128)S(1)} %get-tuple-element.25), channel_id=1, source_target_pairs={{4,0},{8,4},{12,8},{16,12},{20,16},{24,20},{28,24},{5,1},{9,5},{13... | collective-permute-start | bytes 393224 | tf_op jit(solution)/shard_map/ppermute | solution.py:21
  7.9 23.2 %copy-start.6 = (f32[3,65,129]{2,1,0:T(8,128)}, f32[3,65,129]{2,1,0:T(8,128)S(1)}, u32[]{:S(2)}) copy-start(f32[3,65,129]{2,1,0:T(8,128)S(1)} %and_convert_fusion) | copy-start | bytes 301864
  12.0 13.2 %collective-permute-start.2 = (f32[4,4,64,1]{3,2,1,0:T(8,128)S(1)}, f32[4,4,64,1]{3,2,1,0:T(8,128)S(1)}, u32[]{:S(2)}, u32[]{:S(2)}) collective-permute-start(f32[4,4,64,1]{3,2,1,0:T(8,128)S(1)} %get-tuple-element.19), channel_id=1, source_target_pairs={{0,1},{1,2},{2,3},{4,5},{5,6},{6,7},{8,9},{9,10},{10,11},{12,13},{... | collective-permute-start | bytes 12296 | tf_op jit(solution)/shard_map/ppermute | solution.py:18
  15.5 14.4 %collective-permute-start.3 = (f32[4,4,64,1]{3,2,1,0:T(8,128)S(1)}, f32[4,4,64,1]{3,2,1,0:T(8,128)S(1)}, u32[]{:S(2)}, u32[]{:S(2)}) collective-permute-start(f32[4,4,64,1]{3,2,1,0:T(8,128)S(1)} %get-tuple-element.20), channel_id=1, source_target_pairs={{1,0},{2,1},{3,2},{5,4},{6,5},{7,6},{9,8},{10,9},{11,10},{13,12},{... | collective-permute-start | bytes 12296 | tf_op jit(solution)/shard_map/ppermute | solution.py:21
  16.8 14.1 %copy-start.14 = (pred[65]{0:T(512)(128)(4,1)}, pred[65]{0:T(512)(128)(4,1)S(1)}, u32[]{:S(2)}) copy-start(pred[65]{0:T(512)(128)(4,1)S(1)} %fusion.62) | copy-start | bytes 199
  31.7 0.8 copy-start.4
  31.7 0.9 copy-start.9
  32.5 1.5 copy-start
  34.1 2.6 %copy-start.11 = (f32[2,64,128]{2,1,0:T(8,128)}, f32[2,64,128]{2,1,0:T(8,128)S(1)}, u32[]{:S(2)}) copy-start(f32[2,64,128]{2,1,0:T(8,128)S(1)} %maximum_bitcast_fusion.1) | copy-start | bytes 196612
  34.1 58.0 %copy-start.13 = (s32[4]{0:T(128)S(1)}, s32[4]{0:T(128)}, u32[]{:S(2)}) copy-start(s32[4]{0:T(128)} %param.3) | copy-start | bytes 52
  35.2 0.7 copy-start.2
  36.6 50.4 %collective-permute-start.4 = (f32[4,1,64,128]{3,2,1,0:T(8,128)}, f32[4,1,64,128]{3,2,1,0:T(8,128)}, u32[]{:S(2)}, u32[]{:S(2)}) collective-permute-start(f32[4,1,64,128]{3,2,1,0:T(8,128)} %get-tuple-element.22), channel_id=1, source_target_pairs={{0,4},{4,8},{8,12},{12,16},{16,20},{20,24},{24,28},{1,5},{5,9},{9,... | collective-permute-start | bytes 393224 | tf_op jit(solution)/shard_map/ppermute | solution.py:18
  41.3 45.7 %collective-permute-start.5 = (f32[4,1,64,128]{3,2,1,0:T(8,128)}, f32[4,1,64,128]{3,2,1,0:T(8,128)}, u32[]{:S(2)}, u32[]{:S(2)}) collective-permute-start(f32[4,1,64,128]{3,2,1,0:T(8,128)} %get-tuple-element.23), channel_id=1, source_target_pairs={{4,0},{8,4},{12,8},{16,12},{20,16},{24,20},{28,24},{5,1},{9,5},{13... | collective-permute-start | bytes 393224 | tf_op jit(solution)/shard_map/ppermute | solution.py:21
  87.0 5.0 %copy-start.16 = (f32[4]{0:T(128)S(1)}, f32[4]{0:T(128)}, u32[]{:S(2)}) copy-start(f32[4]{0:T(128)} %get-tuple-element.8) | copy-start | bytes 52
  87.0 5.0 %copy-start.17 = (f32[4]{0:T(128)S(1)}, f32[4]{0:T(128)}, u32[]{:S(2)}) copy-start(f32[4]{0:T(128)} %get-tuple-element.9) | copy-start | bytes 52
  87.0 18.4 %copy-start.3 = (f32[4,2,64,128]{3,2,1,0:T(8,128)S(1)}, f32[4,2,64,128]{3,2,1,0:T(8,128)}, u32[]{:S(2)}) copy-start(f32[4,2,64,128]{3,2,1,0:T(8,128)} %copy-done.2) | copy-start | bytes 786436
  88.2 18.8 %copy-start.15 = (pred[65]{0:T(512)(128)(4,1)S(1)}, pred[65]{0:T(512)(128)(4,1)}, u32[]{:S(2)}) copy-start(pred[65]{0:T(512)(128)(4,1)} %copy-done.14) | copy-start | bytes 199
  88.4 12.9 %collective-permute-start.6 = (f32[4,4,64,1]{3,2,1,0:T(8,128)S(1)}, f32[4,4,64,1]{3,2,1,0:T(8,128)S(1)}, u32[]{:S(2)}, u32[]{:S(2)}) collective-permute-start(f32[4,4,64,1]{3,2,1,0:T(8,128)S(1)} %get-tuple-element.17), channel_id=1, source_target_pairs={{0,1},{1,2},{2,3},{4,5},{5,6},{6,7},{8,9},{9,10},{10,11},{12,13},{... | collective-permute-start | bytes 12296 | tf_op jit(solution)/shard_map/ppermute | solution.py:18
  90.7 14.7 %collective-permute-start.7 = (f32[4,4,64,1]{3,2,1,0:T(8,128)S(1)}, f32[4,4,64,1]{3,2,1,0:T(8,128)S(1)}, u32[]{:S(2)}, u32[]{:S(2)}) collective-permute-start(f32[4,4,64,1]{3,2,1,0:T(8,128)S(1)} %get-tuple-element.18), channel_id=1, source_target_pairs={{1,0},{2,1},{3,2},{5,4},{6,5},{7,6},{9,8},{10,9},{11,10},{13,12},{... | collective-permute-start | bytes 12296 | tf_op jit(solution)/shard_map/ppermute | solution.py:21
  107.4 0.9 copy-start.7
  108.8 1.8 %copy-start.1 = (f32[4,3,3,65,129]{4,3,2,0,1:T(8,128)S(1)}, f32[4,3,3,65,129]{4,3,2,0,1:T(8,128)}, u32[]{:S(2)}) copy-start(f32[4,3,3,65,129]{4,3,2,0,1:T(8,128)} %copy-done) | copy-start | bytes 3622324
  108.8 1.7 %copy-start.5 = (f32[2,64,128]{2,1,0:T(8,128)S(1)}, f32[2,64,128]{2,1,0:T(8,128)}, u32[]{:S(2)}) copy-start(f32[2,64,128]{2,1,0:T(8,128)} %param.2) | copy-start | bytes 196612
  108.8 1.7 %copy-start.10 = (f32[2,64,128]{2,1,0:T(8,128)S(1)}, f32[2,64,128]{2,1,0:T(8,128)}, u32[]{:S(2)}) copy-start(f32[2,64,128]{2,1,0:T(8,128)} %copy-done.8) | copy-start | bytes 196612
  108.8 1.7 %copy-start.12 = (f32[2,64,128]{2,1,0:T(8,128)S(1)}, f32[2,64,128]{2,1,0:T(8,128)}, u32[]{:S(2)}) copy-start(f32[2,64,128]{2,1,0:T(8,128)} %copy-done.11) | copy-start | bytes 196612
  112.5 45.9 %all-to-all-start = ((f32[4,2,64,128]{3,1,0,2:T(2,128)}), f32[4,2,64,128]{3,1,0,2:T(2,128)S(1)}, u32[]{:S(2)}, u32[]{:S(2)}) async-start(f32[4,2,64,128]{3,1,0,2:T(2,128)} %copy.8), calls=%async_computation | async-start | bytes 524288 | tf_op jit(solution)/shard_map/all_to_all | solution.py:95
where the time goes:
time: 160 us; the launch traced here: 159 us
  blocking collectives  85.9 us (54%)
  waiting for transfers between devices  30.2 us (19%)
  starting transfers between devices  22 us (14%)
  other arithmetic  12.8 us (8%)
  local copies, waits for them, and re-layouts  7.36 us (5%)
    psum x2, blocking collectives, local(): lax.psum((sizes_local, weighted), ('gx', 'gy', 'gz'))  85.9 us
    ppermute x4, waiting for transfers between devices, with_halo(): lax.ppermute(lax.slice_in_dim(block, block.shape[dim] - width, None, axis...  17.6 us
    ppermute x4, starting transfers between devices, with_halo(): lax.ppermute(lax.slice_in_dim(block, block.shape[dim] - width, None, axis...  12.9 us
    ppermute x4, waiting for transfers between devices, with_halo(): lax.ppermute(lax.slice_in_dim(block, 0, width, axis=dim), axis, backward)  12.6 us
    ppermute x4, starting transfers between devices, with_halo(): lax.ppermute(lax.slice_in_dim(block, 0, width, axis=dim), axis, backward)  5.16 us
    unnamed x36, local copies, waits for them, and re-layouts  4.51 us
    all_to_all x1, starting transfers between devices, local(): lax.all_to_all(labelling, 'gy', split_axis=2, concat_axis=1, tiled=True)  3.9 us
  transfers between devices with their start and end apart: 9, of which 5 were waited for; matrix products, arithmetic and copies ran while one was open for 0% of the time, Pallas kernels for 0%

commit v1 on v0

--- a/solution.py
+++ b/solution.py
@@ -8,6 +8,12 @@
 sigma_step = 0.25
 smooth_weight = 0.5
 prior_weight = 1.0
+
+
+def find_the_meshes(z_in):
+    for jj in ("gx", ("gy", "gz")):
+        z_in = lax.psum(z_in, axis_name=jj)
+    return z_in
 
 
 def with_halo(block, sides, width):
@@ -90,7 +96,7 @@
         labelling = updated
         sizes_local = jnp.sum(labelling, axis=(1, 2, 3))
         weighted = jnp.sum(labelling * volume[None], axis=(1, 2, 3))
-        sizes_all, weighted_all = lax.psum((sizes_local, weighted), ("gx", "gy", "gz"))
+        sizes_all, weighted_all = find_the_meshes((sizes_local, weighted))
         centers = (weighted_all + prior_weight * base_levels) / (sizes_all + prior_weight)
     labelling = lax.all_to_all(labelling, "gy", split_axis=2, concat_axis=1, tiled=True)
     return (labelling, centers)

time: 160 us -> 149 us (0.931)
  blocking collectives: 85.9 us -> 77.6 us
  waiting for transfers between devices: 30.2 us -> 27.4 us
    psum x2 -> x4, blocking collectives: 85.9 us -> 77.6 us  [find_the_meshes(): z_in = lax.psum(z_in, axis_name=jj)]
    ppermute x4, waiting for transfers between devices: 17.6 us -> 14.8 us  [with_halo(): lax.ppermute(lax.slice_in_dim(block, block.shape[dim] - width, None, axis...]
  transfers between devices with their start and end apart: 9 -> 9, of which waited for: 5 -> 5; matrix products, arithmetic and copies ran while one was open for 0% -> 1% of each run, Pallas kernels for 0% -> 0%
where the time goes in v1:
time: 149 us; the launch traced here: 148 us
  blocking collectives  77.6 us (52%)
  waiting for transfers between devices  27.4 us (18%)
  starting transfers between devices  21.8 us (15%)
  other arithmetic  12.8 us (9%)
  local copies, waits for them, and re-layouts  7.37 us (5%)
    psum x4, blocking collectives, find_the_meshes(): z_in = lax.psum(z_in, axis_name=jj)  77.6 us
    ppermute x4, waiting for transfers between devices, with_halo(): lax.ppermute(lax.slice_in_dim(block, block.shape[dim] - width, None, axis...  14.8 us
    ppermute x4, starting transfers between devices, with_halo(): lax.ppermute(lax.slice_in_dim(block, block.shape[dim] - width, None, axis...  13.2 us
    ppermute x4, waiting for transfers between devices, with_halo(): lax.ppermute(lax.slice_in_dim(block, 0, width, axis=dim), axis, backward)  12.6 us
    ppermute x4, starting transfers between devices, with_halo(): lax.ppermute(lax.slice_in_dim(block, 0, width, axis=dim), axis, backward)  5.16 us
    unnamed x36, local copies, waits for them, and re-layouts  4.52 us
    all_to_all x1, starting transfers between devices, local(): lax.all_to_all(labelling, 'gy', split_axis=2, concat_axis=1, tiled=True)  3.41 us
    concatenate x4, other arithmetic, with_halo(): block = jnp.concatenate([low, block, high], axis=dim)  3.2 us
  transfers between devices with their start and end apart: 9, of which 5 were waited for; matrix products, arithmetic and copies ran while one was open for 1% of the time, Pallas kernels for 0%

profile of v1, /device:TPU:0, one launch (start us, length us, event | category | flops | bytes accessed | tf_op | source)
XLA Modules:
  0.0 147.9 jit_solution(249447750562619487)
XLA Ops:
  0.6 0.7 convert_multiply_fusion
  1.3 0.9 multiply_subtract_fusion.1
  2.2 0.1 maximum_bitcast_fusion.2
  2.4 0.6 copy-done.8
  3.0 1.0 subtract_maximum_fusion.2
  4.0 2.4 %collective-permute-start = (f32[4,1,64,128]{3,2,1,0:T(8,128)S(1)}, f32[4,1,64,128]{3,2,1,0:T(8,128)S(1)}, u32[]{:S(2)}, u32[]{:S(2)}) collective-permute-start(f32[4,1,64,128]{3,2,1,0:T(8,128)S(1)} %get-tuple-element.28), channel_id=1, source_target_pairs={{0,4},{4,8},{8,12},{12,16},{16,20},{20,24},{24,28},{1,5},{5,9},{9,... | collective-permute-start | bytes 393224 | tf_op jit(solution)/shard_map/ppermute | solution.py:24
  6.4 1.3 collective-permute-start.1
  7.8 0.1 broadcast_and_fusion
  7.8 0.1 and_convert_fusion
  8.0 0.0 collective-permute-done
  8.0 3.7 %collective-permute-done.1 = f32[4,1,64,128]{3,2,1,0:T(8,128)S(1)} collective-permute-done((f32[4,1,64,128]{3,2,1,0:T(8,128)S(1)}, f32[4,1,64,128]{3,2,1,0:T(8,128)S(1)}, u32[]{:S(2)}, u32[]{:S(2)}) %collective-permute-start.1) | collective-permute-done | bytes 131104 | tf_op jit(solution)/shard_map/ppermute | solution.py:27
  11.8 0.2 fusion.66
  12.0 3.5 %collective-permute-start.2 = (f32[4,4,64,1]{3,2,1,0:T(8,128)S(1)}, f32[4,4,64,1]{3,2,1,0:T(8,128)S(1)}, u32[]{:S(2)}, u32[]{:S(2)}) collective-permute-start(f32[4,4,64,1]{3,2,1,0:T(8,128)S(1)} %get-tuple-element.23), channel_id=1, source_target_pairs={{0,1},{1,2},{2,3},{4,5},{5,6},{6,7},{8,9},{9,10},{10,11},{12,13},{... | collective-permute-start | bytes 12296 | tf_op jit(solution)/shard_map/ppermute | solution.py:24
  15.5 1.3 collective-permute-start.3
  16.8 0.0 copy-start.14
  16.8 8.4 %collective-permute-done.2 = f32[4,4,64,1]{3,2,1,0:T(8,128)S(1)} collective-permute-done((f32[4,4,64,1]{3,2,1,0:T(8,128)S(1)}, f32[4,4,64,1]{3,2,1,0:T(8,128)S(1)}, u32[]{:S(2)}, u32[]{:S(2)}) %collective-permute-start.2) | collective-permute-done | bytes 4128 | tf_op jit(solution)/shard_map/ppermute | solution.py:24
  25.2 4.7 %collective-permute-done.3 = f32[4,4,64,1]{3,2,1,0:T(8,128)S(1)} collective-permute-done((f32[4,4,64,1]{3,2,1,0:T(8,128)S(1)}, f32[4,4,64,1]{3,2,1,0:T(8,128)S(1)}, u32[]{:S(2)}, u32[]{:S(2)}) %collective-permute-start.3) | collective-permute-done | bytes 4128 | tf_op jit(solution)/shard_map/ppermute | solution.py:27
  29.9 0.5 select_maximum_fusion.4
  30.4 0.5 fusion.29
  30.9 0.2 fusion.2
  31.2 0.5 fusion.30
  31.7 0.0 copy-start.4
  31.7 0.3 fusion.1
  32.0 0.5 copy-done.4
  32.5 0.0 copy-done.9
  32.6 0.5 fusion.41
  33.0 0.1 maximum_bitcast_fusion.1
  33.1 0.9 copy-done
  34.1 1.2 multiply_reduce_fusion.1
  35.2 0.7 copy-done.2
  35.9 0.7 fusion.67
  36.7 4.7 %collective-permute-start.4 = (f32[4,1,64,128]{3,2,1,0:T(8,128)}, f32[4,1,64,128]{3,2,1,0:T(8,128)}, u32[]{:S(2)}, u32[]{:S(2)}) collective-permute-start(f32[4,1,64,128]{3,2,1,0:T(8,128)} %get-tuple-element.26), channel_id=1, source_target_pairs={{0,4},{4,8},{8,12},{12,16},{16,20},{20,24},{24,28},{1,5},{5,9},{9,... | collective-permute-start | bytes 393224 | tf_op jit(solution)/shard_map/ppermute | solution.py:24
  41.3 1.3 collective-permute-start.5
  42.6 10.2 %all-reduce.5 = (f32[4]{0:T(128)}, f32[4]{0:T(128)}) all-reduce(f32[4]{0:T(128)} %get-tuple-element.3, f32[4]{0:T(128)} %get-tuple-element.2), channel_id=1, replica_groups=mesh['gx'=2,'gy'=4,'gz'=4] {'gx'}, use_global_device_ids=true, to_apply=%region_4.5 | all-reduce | flops 8 | bytes 64 | tf_op jit(solution)/shard_map/psum | solution.py:15
  52.8 31.9 %all-reduce.3 = (f32[4]{0:T(128)}, f32[4]{0:T(128)}) all-reduce(f32[4]{0:T(128)} %get-tuple-element.12, f32[4]{0:T(128)} %get-tuple-element.13), channel_id=1, replica_groups=mesh['gx'=2,'gy'=4,'gz'=4] {'gy','gz'}, use_global_device_ids=true, to_apply=%region_5.6 | all-reduce | flops 8 | bytes 64 | tf_op jit(solution)/shard_map/psum | solution.py:15
  84.7 0.0 collective-permute-done.4
  84.7 0.0 collective-permute-done.5
  84.7 1.1 pad_maximum_fusion.2
  85.8 0.2 fusion.65
  86.1 2.7 %collective-permute-start.6 = (f32[4,4,64,1]{3,2,1,0:T(8,128)S(1)}, f32[4,4,64,1]{3,2,1,0:T(8,128)S(1)}, u32[]{:S(2)}, u32[]{:S(2)}) collective-permute-start(f32[4,4,64,1]{3,2,1,0:T(8,128)S(1)} %get-tuple-element.21), channel_id=1, source_target_pairs={{0,1},{1,2},{2,3},{4,5},{5,6},{6,7},{8,9},{9,10},{10,11},{12,13},{... | collective-permute-start | bytes 12296 | tf_op jit(solution)/shard_map/ppermute | solution.py:24
  88.7 1.3 collective-permute-start.7
  90.1 6.4 %collective-permute-done.6 = f32[4,4,64,1]{3,2,1,0:T(8,128)S(1)} collective-permute-done((f32[4,4,64,1]{3,2,1,0:T(8,128)S(1)}, f32[4,4,64,1]{3,2,1,0:T(8,128)S(1)}, u32[]{:S(2)}, u32[]{:S(2)}) %collective-permute-start.6) | collective-permute-done | bytes 4128 | tf_op jit(solution)/shard_map/ppermute | solution.py:24
  96.4 4.1 %collective-permute-done.7 = f32[4,4,64,1]{3,2,1,0:T(8,128)S(1)} collective-permute-done((f32[4,4,64,1]{3,2,1,0:T(8,128)S(1)}, f32[4,4,64,1]{3,2,1,0:T(8,128)S(1)}, u32[]{:S(2)}, u32[]{:S(2)}) %collective-permute-start.7) | collective-permute-done | bytes 4128 | tf_op jit(solution)/shard_map/ppermute | solution.py:27
  100.6 1.5 %select_maximum_fusion = f32[4,4,66,130]{3,2,1,0:T(8,128)S(1)} fusion(f32[4,4,64,1]{3,2,1,0:T(8,128)S(1)} %collective-permute-done.7, f32[4,4,64,1]{3,2,1,0:T(8,128)S(1)} %collective-permute-done.6, f32[4,1,64,128]{3,2,1,0:T(8,128)} %collective-permute-done.5, f32[4,2,64,128]{3,2,1,0:T(8,128)S(1)} %copy-done.3, f32[4,1,64,128]{3,2,1,0:T(8,128)} %collective-permute-done.4), kind=kLoop, calls=%fused_computation.8 | loop fusion | flops 1647360 | bytes 1081600 | tf_op jit(solution)/shard_map/concatenate | solution.py:28
  102.1 0.4 fusion.16
  102.6 0.4 fusion
  103.0 0.5 copy-done.7
  103.5 0.5 fusion.9
  104.0 0.0 copy-start.5
  104.0 0.5 broadcast_multiply_fusion
  104.5 1.2 copy-done.1
  105.7 0.0 copy-done.5
  105.7 0.0 copy-done.12
  105.7 0.8 fusion.35
  106.5 0.1 maximum_bitcast_fusion
  106.6 0.2 multiply_reduce_fusion
  106.8 0.9 copy.8
  107.7 3.4 %all-to-all-start = ((f32[4,2,64,128]{3,1,0,2:T(2,128)}), f32[4,2,64,128]{3,1,0,2:T(2,128)S(1)}, u32[]{:S(2)}, u32[]{:S(2)}) async-start(f32[4,2,64,128]{3,1,0,2:T(2,128)} %copy.8), calls=%async_computation | async-start | bytes 524288 | tf_op jit(solution)/shard_map/all_to_all | solution.py:101
  111.1 4.9 %all-reduce.4 = (f32[4]{0:T(128)S(1)}, f32[4]{0:T(128)S(1)}) all-reduce(f32[4]{0:T(128)S(1)} %get-tuple-element.5, f32[4]{0:T(128)S(1)} %get-tuple-element.4), channel_id=1, replica_groups=mesh['gx'=2,'gy'=4,'gz'=4] {'gx'}, use_global_device_ids=true, to_apply=%region_10.11 | all-reduce | flops 8 | bytes 64 | tf_op jit(solution)/shard_map/psum | solution.py:15
  116.0 30.6 %all-reduce.2 = (f32[4]{0:T(128)S(1)}, f32[4]{0:T(128)S(1)}) all-reduce(f32[4]{0:T(128)S(1)} %get-tuple-element.10, f32[4]{0:T(128)S(1)} %get-tuple-element.11), channel_id=1, replica_groups=mesh['gx'=2,'gy'=4,'gz'=4] {'gy','gz'}, use_global_device_ids=true, to_apply=%region_11.12 | all-reduce | flops 8 | bytes 64 | tf_op jit(solution)/shard_map/psum | solution.py:15
  146.6 0.5 add_divide_fusion
  147.1 0.0 all-to-all-done
  147.2 0.1 copy.9
  147.2 0.7 copy.10
  (33 shorter events, 0.2 us)
Async XLA Ops:
  2.4 0.6 copy-start.8
  4.0 4.0 %collective-permute-start = (f32[4,1,64,128]{3,2,1,0:T(8,128)S(1)}, f32[4,1,64,128]{3,2,1,0:T(8,128)S(1)}, u32[]{:S(2)}, u32[]{:S(2)}) collective-permute-start(f32[4,1,64,128]{3,2,1,0:T(8,128)S(1)} %get-tuple-element.28), channel_id=1, source_target_pairs={{0,4},{4,8},{8,12},{12,16},{16,20},{20,24},{24,28},{1,5},{5,9},{9,... | collective-permute-start | bytes 393224 | tf_op jit(solution)/shard_map/ppermute | solution.py:24
  6.4 5.3 %collective-permute-start.1 = (f32[4,1,64,128]{3,2,1,0:T(8,128)S(1)}, f32[4,1,64,128]{3,2,1,0:T(8,128)S(1)}, u32[]{:S(2)}, u32[]{:S(2)}) collective-permute-start(f32[4,1,64,128]{3,2,1,0:T(8,128)S(1)} %get-tuple-element.29), channel_id=1, source_target_pairs={{4,0},{8,4},{12,8},{16,12},{20,16},{24,20},{28,24},{5,1},{9,5},{13... | collective-permute-start | bytes 393224 | tf_op jit(solution)/shard_map/ppermute | solution.py:27
  7.9 23.2 %copy-start.6 = (f32[3,65,129]{2,1,0:T(8,128)}, f32[3,65,129]{2,1,0:T(8,128)S(1)}, u32[]{:S(2)}) copy-start(f32[3,65,129]{2,1,0:T(8,128)S(1)} %and_convert_fusion) | copy-start | bytes 301864
  12.0 13.2 %collective-permute-start.2 = (f32[4,4,64,1]{3,2,1,0:T(8,128)S(1)}, f32[4,4,64,1]{3,2,1,0:T(8,128)S(1)}, u32[]{:S(2)}, u32[]{:S(2)}) collective-permute-start(f32[4,4,64,1]{3,2,1,0:T(8,128)S(1)} %get-tuple-element.23), channel_id=1, source_target_pairs={{0,1},{1,2},{2,3},{4,5},{5,6},{6,7},{8,9},{9,10},{10,11},{12,13},{... | collective-permute-start | bytes 12296 | tf_op jit(solution)/shard_map/ppermute | solution.py:24
  15.5 14.4 %collective-permute-start.3 = (f32[4,4,64,1]{3,2,1,0:T(8,128)S(1)}, f32[4,4,64,1]{3,2,1,0:T(8,128)S(1)}, u32[]{:S(2)}, u32[]{:S(2)}) collective-permute-start(f32[4,4,64,1]{3,2,1,0:T(8,128)S(1)} %get-tuple-element.24), channel_id=1, source_target_pairs={{1,0},{2,1},{3,2},{5,4},{6,5},{7,6},{9,8},{10,9},{11,10},{13,12},{... | collective-permute-start | bytes 12296 | tf_op jit(solution)/shard_map/ppermute | solution.py:27
  16.8 14.1 %copy-start.14 = (pred[65]{0:T(512)(128)(4,1)}, pred[65]{0:T(512)(128)(4,1)S(1)}, u32[]{:S(2)}) copy-start(pred[65]{0:T(512)(128)(4,1)S(1)} %fusion.62) | copy-start | bytes 199
  31.7 0.8 copy-start.4
  31.7 0.9 copy-start.9
  32.6 1.5 %copy-start = (f32[4,3,3,65,129]{4,3,2,0,1:T(8,128)}, f32[4,3,3,65,129]{4,3,2,0,1:T(8,128)S(1)}, u32[]{:S(2)}) copy-start(f32[4,3,3,65,129]{4,3,2,0,1:T(8,128)S(1)} %fusion.1) | copy-start | bytes 3622324
  34.1 2.6 %copy-start.11 = (f32[2,64,128]{2,1,0:T(8,128)}, f32[2,64,128]{2,1,0:T(8,128)S(1)}, u32[]{:S(2)}) copy-start(f32[2,64,128]{2,1,0:T(8,128)S(1)} %maximum_bitcast_fusion.1) | copy-start | bytes 196612
  34.1 55.9 %copy-start.13 = (s32[4]{0:T(128)S(1)}, s32[4]{0:T(128)}, u32[]{:S(2)}) copy-start(s32[4]{0:T(128)} %param.3) | copy-start | bytes 52
  35.2 0.7 copy-start.2
  36.7 48.0 %collective-permute-start.4 = (f32[4,1,64,128]{3,2,1,0:T(8,128)}, f32[4,1,64,128]{3,2,1,0:T(8,128)}, u32[]{:S(2)}, u32[]{:S(2)}) collective-permute-start(f32[4,1,64,128]{3,2,1,0:T(8,128)} %get-tuple-element.26), channel_id=1, source_target_pairs={{0,4},{4,8},{8,12},{12,16},{16,20},{20,24},{24,28},{1,5},{5,9},{9,... | collective-permute-start | bytes 393224 | tf_op jit(solution)/shard_map/ppermute | solution.py:24
  41.3 43.4 %collective-permute-start.5 = (f32[4,1,64,128]{3,2,1,0:T(8,128)}, f32[4,1,64,128]{3,2,1,0:T(8,128)}, u32[]{:S(2)}, u32[]{:S(2)}) collective-permute-start(f32[4,1,64,128]{3,2,1,0:T(8,128)} %get-tuple-element.27), channel_id=1, source_target_pairs={{4,0},{8,4},{12,8},{16,12},{20,16},{24,20},{28,24},{5,1},{9,5},{13... | collective-permute-start | bytes 393224 | tf_op jit(solution)/shard_map/ppermute | solution.py:27
  84.7 5.4 %copy-start.16 = (f32[4]{0:T(128)S(1)}, f32[4]{0:T(128)}, u32[]{:S(2)}) copy-start(f32[4]{0:T(128)} %get-tuple-element.8) | copy-start | bytes 52
  84.7 5.4 %copy-start.17 = (f32[4]{0:T(128)S(1)}, f32[4]{0:T(128)}, u32[]{:S(2)}) copy-start(f32[4]{0:T(128)} %get-tuple-element.9) | copy-start | bytes 52
  84.7 15.9 %copy-start.3 = (f32[4,2,64,128]{3,2,1,0:T(8,128)S(1)}, f32[4,2,64,128]{3,2,1,0:T(8,128)}, u32[]{:S(2)}) copy-start(f32[4,2,64,128]{3,2,1,0:T(8,128)} %copy-done.2) | copy-start | bytes 786436
  85.8 16.3 %copy-start.15 = (pred[65]{0:T(512)(128)(4,1)S(1)}, pred[65]{0:T(512)(128)(4,1)}, u32[]{:S(2)}) copy-start(pred[65]{0:T(512)(128)(4,1)} %copy-done.14) | copy-start | bytes 199
  86.1 10.4 %collective-permute-start.6 = (f32[4,4,64,1]{3,2,1,0:T(8,128)S(1)}, f32[4,4,64,1]{3,2,1,0:T(8,128)S(1)}, u32[]{:S(2)}, u32[]{:S(2)}) collective-permute-start(f32[4,4,64,1]{3,2,1,0:T(8,128)S(1)} %get-tuple-element.21), channel_id=1, source_target_pairs={{0,1},{1,2},{2,3},{4,5},{5,6},{6,7},{8,9},{9,10},{10,11},{12,13},{... | collective-permute-start | bytes 12296 | tf_op jit(solution)/shard_map/ppermute | solution.py:24
  88.7 11.9 %collective-permute-start.7 = (f32[4,4,64,1]{3,2,1,0:T(8,128)S(1)}, f32[4,4,64,1]{3,2,1,0:T(8,128)S(1)}, u32[]{:S(2)}, u32[]{:S(2)}) collective-permute-start(f32[4,4,64,1]{3,2,1,0:T(8,128)S(1)} %get-tuple-element.22), channel_id=1, source_target_pairs={{1,0},{2,1},{3,2},{5,4},{6,5},{7,6},{9,8},{10,9},{11,10},{13,12},{... | collective-permute-start | bytes 12296 | tf_op jit(solution)/shard_map/ppermute | solution.py:27
  102.5 0.9 copy-start.7
  104.0 1.8 %copy-start.1 = (f32[4,3,3,65,129]{4,3,2,0,1:T(8,128)S(1)}, f32[4,3,3,65,129]{4,3,2,0,1:T(8,128)}, u32[]{:S(2)}) copy-start(f32[4,3,3,65,129]{4,3,2,0,1:T(8,128)} %copy-done) | copy-start | bytes 3622324
  104.0 1.7 %copy-start.5 = (f32[2,64,128]{2,1,0:T(8,128)S(1)}, f32[2,64,128]{2,1,0:T(8,128)}, u32[]{:S(2)}) copy-start(f32[2,64,128]{2,1,0:T(8,128)} %param.2) | copy-start | bytes 196612
  104.0 1.7 %copy-start.10 = (f32[2,64,128]{2,1,0:T(8,128)S(1)}, f32[2,64,128]{2,1,0:T(8,128)}, u32[]{:S(2)}) copy-start(f32[2,64,128]{2,1,0:T(8,128)} %copy-done.8) | copy-start | bytes 196612
  104.0 1.7 %copy-start.12 = (f32[2,64,128]{2,1,0:T(8,128)S(1)}, f32[2,64,128]{2,1,0:T(8,128)}, u32[]{:S(2)}) copy-start(f32[2,64,128]{2,1,0:T(8,128)} %copy-done.11) | copy-start | bytes 196612
  107.7 39.5 %all-to-all-start = ((f32[4,2,64,128]{3,1,0,2:T(2,128)}), f32[4,2,64,128]{3,1,0,2:T(2,128)S(1)}, u32[]{:S(2)}, u32[]{:S(2)}) async-start(f32[4,2,64,128]{3,1,0,2:T(2,128)} %copy.8), calls=%async_computation | async-start | bytes 524288 | tf_op jit(solution)/shard_map/all_to_all | solution.py:101
